TPU v7x, 256 devices: a whole 4x4x8 slice. The times are simulated.
256 devices in a mesh: gx: 16 (over z, x_lo), gy: 16 (over y, x_hi, core).
Axes of the slice: x: 4 (x_hi: 2, x_lo: 2; x = x_hi * 2 + x_lo), y: 4, z: 8, core: 2. Of those that a mesh axis runs over, the one named last changes fastest.
Arguments:
- gradient: float32 [2048, 512], P('gx', 'gy'), may hold values from -6 to 6
- stat_old: float32 [2048, 2048], P('gx', 'gy'), may hold values from -1.001 to 1.001, as said below
Outputs:
- statistic: float32 [2048, 2048], P('gx', 'gy')
- inverse_root: float32 [2048, 2048], P('gx', 'gy')
Inputs may be any that keep to these rules, and one draw needn't show every extreme that they name: stat_old is symmetric positive semidefinite with unit diagonal, the Gram matrix of 2048 unit-length rows of 512 entries.
All inputs are finite; a program needn't handle non-finite values.
Results may differ from a plain program's by a relative error of at most 0.0003.
Values sent between devices are 32-bit elements.
A program may use at most 64 MiB of HBM per device.

v0:
```python
import jax
import jax.numpy as jnp
from jax import lax
from jax.sharding import Mesh
from jax.sharding import PartitionSpec as P

GY = ("gy_0", "gy_1", "gy_2")
GX = ("gx_0", "gx_1")
GX_GY = ("gx_0", "gx_1", "gy_0", "gy_1", "gy_2")


def gather_axes(array, axes, dim):
    filled = array
    for number in range(len(axes) - 1, -1, -1):
        filled = lax.all_gather(filled, axes[number], axis=dim, tiled=True)
    return filled


def folded(array, axes, dim, take_in, carry):
    everything = jax.tree.map(lambda part: gather_axes(part, axes, dim), array)
    return take_in(carry, everything, jnp.int32(0))


def spread(array, axes, root):
    array = jnp.where(lax.axis_index(axes) == root, array, jnp.zeros_like(array))
    for axis in axes:
        array = lax.psum(array, axis)
    return array


def over_axes(array, axes):
    for axis in axes:
        array = lax.psum(array, axis)
    return array


def matmul(leading, trailing):
    return jnp.dot(
        leading, trailing, preferred_element_type=jnp.float32, precision=lax.Precision.HIGHEST
    )


def panels(factor_one, factor_two):
    whole_row = lax.all_gather(factor_one, GY, axis=1, tiled=True)

    def accumulate(running, shard_rows, first_row):
        matching = lax.dynamic_slice_in_dim(whole_row, first_row, shard_rows.shape[0], 1)
        return running + matmul(matching, shard_rows)

    empty = jnp.zeros((factor_one.shape[0], factor_two.shape[1]), jnp.float32)
    return folded(factor_two, GX, 0, accumulate, empty)


def product(factor_one, factor_two):
    return panels(factor_one, factor_two)


def local(gradient, stat_old):
    count_rows = lax.axis_size(GX)
    count_cols = lax.axis_size(GY)
    factor = count_rows // count_cols
    piece_width = stat_old.shape[0]
    row_index = lax.axis_index(GX)
    col_index = lax.axis_index(GY)
    panel_rows = lax.all_gather(gradient, GY, axis=1, tiled=True)
    outer_parts = []
    for member in range(factor):
        column_rows = spread(panel_rows, GX, col_index * factor + member)
        outer_parts.append(matmul(panel_rows, column_rows.T))
    outer = jnp.concatenate(outer_parts, axis=1) / panel_rows.shape[1]
    statistic = 0.9 * stat_old + outer
    squares = over_axes(jnp.sum(statistic * statistic), GX_GY)
    divisor = 2.0 * jnp.sqrt(squares / (piece_width * count_rows))
    global_rows = row_index * piece_width + lax.broadcasted_iota(jnp.int32, stat_old.shape, 0)
    global_cols = col_index * (factor * piece_width) + lax.broadcasted_iota(
        jnp.int32, stat_old.shape, 1
    )
    identity = (global_rows == global_cols).astype(jnp.float32)
    normed = statistic / divisor
    first_step = 1.5 * identity - 0.5 * normed
    root_half = product(normed, first_step)
    product_mid = product(first_step, root_half)
    second_step = 1.5 * identity - 0.5 * product_mid
    inverse_root = product(second_step, first_step)
    return (statistic, inverse_root)


def solution(mesh):
    torus = Mesh(mesh.devices.reshape(8, 2, 4, 2, 2), ("gx_0", "gx_1", "gy_0", "gy_1", "gy_2"))
    placed = (P(GX, GY), P(GX, GY))
    return jax.shard_map(
        local, mesh=torus, in_specs=placed, out_specs=(P(GX, GY), P(GX, GY)), check_vma=False
    )
```

profile of v0, /device:TPU:1, one launch (start us, length us, event | category | flops | bytes accessed | tf_op | source)
XLA Modules:
  0.0 435.5 jit_solution(8363940582427046131)
XLA Ops:
  7.2 0.0 copy-start.3
  7.2 0.0 all-reduce.3.cloned.1.call-start
  7.2 0.7 copy-done.3
  7.9 26.8 %all_gather.26 = f32[128,512]{0,1:T(8,128)S(1)} all-gather(f32[128,32]{0,1:T(8,128)S(1)} %copy-done.3), channel_id=1, replica_groups=mesh['gx_0'=8,'gx_1'=2,'gy_0'=4,'gy_1'=2,'gy_2'=2] {'gy_0','gy_1','gy_2'}, dimensions={1}, use_global_device_ids=true | all-gather | bytes 278528 | tf_op jit(solution)/shard_map/all_gather | solution.py:65
  34.6 0.7 broadcast_select_fusion
  35.4 0.0 all-reduce.3.cloned.1.call-update
  35.4 0.0 all-reduce.5.cloned.1.call-start
  35.4 65.4 %all-reduce.3.cloned.1.call-done = f32[128,512]{0,1:T(8,128)} async-done(((f32[128,512]{0,1:T(8,128)}), f32[128,512]{0,1:T(8,128)}) %all-reduce.3.cloned.1.call-update) | async-done | bytes 262160 | tf_op jit(solution)/shard_map/psum | solution.py:27
  100.8 0.0 copy-start.2
  100.8 0.0 all-reduce.5.cloned.1.call-update
  100.8 0.0 all-gather.10.cloned.1.call-start
  100.9 0.8 copy-done.2
  101.6 0.1 copy.4
  101.7 39.7 %all-reduce.5.cloned.1.call-done = f32[128,512]{0,1:T(8,128)} async-done(((f32[128,512]{0,1:T(8,128)}), f32[128,512]{0,1:T(8,128)}) %all-reduce.5.cloned.1.call-update) | async-done | bytes 262160 | tf_op jit(solution)/shard_map/psum | solution.py:27
  141.4 2.1 multiply_reduce_fusion
  143.6 14.6 %psum.51 = f32[]{:T(128)} all-reduce(f32[]{:T(128)} %get-tuple-element.6), channel_id=1, replica_groups=mesh['gx_0'=8,'gx_1'=2,'gy_0'=4,'gy_1'=2,'gy_2'=2] {'gx_0'}, use_global_device_ids=true, to_apply=%region_3.4 | all-reduce | flops 1 | bytes 8 | tf_op jit(solution)/shard_map/psum | solution.py:33
  158.1 4.4 %psum.52 = f32[]{:T(128)} all-reduce(f32[]{:T(128)} %psum.51), channel_id=1, replica_groups=mesh['gx_0'=8,'gx_1'=2,'gy_0'=4,'gy_1'=2,'gy_2'=2] {'gx_1'}, use_global_device_ids=true, to_apply=%region_4.5 | all-reduce | flops 1 | bytes 8 | tf_op jit(solution)/shard_map/psum | solution.py:33
  162.5 9.1 %psum.53 = f32[]{:T(128)} all-reduce(f32[]{:T(128)} %psum.52), channel_id=1, replica_groups=mesh['gx_0'=8,'gx_1'=2,'gy_0'=4,'gy_1'=2,'gy_2'=2] {'gy_0'}, use_global_device_ids=true, to_apply=%region_5.6 | all-reduce | flops 1 | bytes 8 | tf_op jit(solution)/shard_map/psum | solution.py:33
  171.6 5.9 %psum.54 = f32[]{:T(128)} all-reduce(f32[]{:T(128)} %psum.53), channel_id=1, replica_groups=mesh['gx_0'=8,'gx_1'=2,'gy_0'=4,'gy_1'=2,'gy_2'=2] {'gy_1'}, use_global_device_ids=true, to_apply=%region_6.7 | all-reduce | flops 1 | bytes 8 | tf_op jit(solution)/shard_map/psum | solution.py:33
  177.5 11.8 %psum.55 = f32[]{:T(128)} all-reduce(f32[]{:T(128)} %psum.54), channel_id=1, replica_groups=mesh['gx_0'=8,'gx_1'=2,'gy_0'=4,'gy_1'=2,'gy_2'=2] {'gy_2'}, use_global_device_ids=true, to_apply=%region_7.8 | all-reduce | flops 1 | bytes 8 | tf_op jit(solution)/shard_map/psum | solution.py:33
  190.0 0.6 select_subtract_fusion
  190.6 0.0 copy-start.1
  190.6 3.9 all_gather.29
  194.5 0.0 copy-done.1
  194.5 0.0 all-gather.10.cloned.1.call-update
  194.5 0.0 all-gather.8.cloned.1.call-start
  194.6 0.5 all-gather.8.cloned.1.call-update
  195.1 0.0 all-gather.6.cloned.1.call-start
  195.1 0.5 all-gather.6.cloned.1.call-update
  195.7 0.0 all-gather.12.cloned.1.call-start
  195.7 29.4 %all-gather.10.cloned.1.call-done = f32[2048,128]{0,1:T(8,128)} async-done(((f32[256,128]{0,1:T(8,128)}), f32[2048,128]{0,1:T(8,128)}) %all-gather.10.cloned.1.call-update) | async-done | bytes 1048592 | tf_op jit(solution)/shard_map/all_gather | solution.py:15
  225.1 56.8 %all-gather.8.cloned.1.call-done = f32[128,2048]{0,1:T(8,128)} async-done(((f32[128,128]{0,1:T(8,128)}), f32[128,2048]{0,1:T(8,128)}) %all-gather.8.cloned.1.call-update) | async-done | bytes 1048592 | tf_op jit(solution)/shard_map/all_gather | solution.py:44
  281.9 3.4 fusion.3
  285.2 3.9 all_gather.31
  289.1 0.0 all-gather.12.cloned.1.call-update
  289.1 0.0 copy-start
  289.1 0.0 all-gather.14.cloned.1.call-start
  289.2 44.5 %all-gather.6.cloned.1.call-done = f32[128,2048]{0,1:T(8,128)} async-done(((f32[128,128]{0,1:T(8,128)}), f32[128,2048]{0,1:T(8,128)}) %all-gather.6.cloned.1.call-update) | async-done | bytes 1048592 | tf_op jit(solution)/shard_map/all_gather | solution.py:44
  333.7 33.6 %all-gather.12.cloned.1.call-done = f32[2048,128]{1,0:T(8,128)} async-done(((f32[256,128]{1,0:T(8,128)}), f32[2048,128]{1,0:T(8,128)}) %all-gather.12.cloned.1.call-update) | async-done | bytes 1048592 | tf_op jit(solution)/shard_map/all_gather | solution.py:15
  367.3 4.0 fusion
  371.3 0.0 all-gather.14.cloned.1.call-update
  371.3 0.7 copy.5
  372.0 53.0 %all-gather.14.cloned.1.call-done = f32[128,2048]{0,1:T(8,128)} async-done(((f32[128,128]{0,1:T(8,128)}), f32[128,2048]{0,1:T(8,128)}) %all-gather.14.cloned.1.call-update) | async-done | bytes 1048592 | tf_op jit(solution)/shard_map/all_gather | solution.py:44
  425.0 0.0 copy-done
  425.0 3.7 fusion.4
  (1 shorter events, 0.0 us)
Async XLA Ops:
  7.2 0.7 copy-start.3
  7.2 93.6 %all-reduce.3.cloned.1.call-start = ((), (), s32[]{:S(2)}) async-start(), calls=%async_computation | async-start | bytes 524288 | tf_op jit(solution)/shard_map/psum | solution.py:27
  35.4 106.1 %all-reduce.5.cloned.1.call-start = ((), (), s32[]{:S(2)}) async-start(), calls=%async_computation.1 | async-start | bytes 524288 | tf_op jit(solution)/shard_map/psum | solution.py:27
  100.8 0.8 copy-start.2
  100.8 124.2 %all-gather.10.cloned.1.call-start = ((), (), s32[]{:S(2)}) async-start(), calls=%async_computation.4 | async-start | bytes 1179648 | tf_op jit(solution)/shard_map/all_gather | solution.py:15
  190.6 3.9 copy-start.1
  194.5 87.3 %all-gather.8.cloned.1.call-start = ((), (), s32[]{:S(2)}) async-start(), calls=%async_computation.3 | async-start | bytes 1114112 | tf_op jit(solution)/shard_map/all_gather | solution.py:44
  195.1 138.6 %all-gather.6.cloned.1.call-start = ((), (), s32[]{:S(2)}) async-start(), calls=%async_computation.2 | async-start | bytes 1114112 | tf_op jit(solution)/shard_map/all_gather | solution.py:44
  195.7 171.6 %all-gather.12.cloned.1.call-start = ((), (), s32[]{:S(2)}) async-start(), calls=%async_computation.5 | async-start | bytes 1179648 | tf_op jit(solution)/shard_map/all_gather | solution.py:15
  289.1 135.9 %copy-start = (f32[2048,128]{0,1:T(8,128)S(1)}, f32[2048,128]{0,1:T(8,128)}, u32[]{:S(2)}) copy-start(f32[2048,128]{0,1:T(8,128)} %all-gather.10.cloned.1.call-done) | copy-start | bytes 3145732
  289.1 135.9 %all-gather.14.cloned.1.call-start = ((), (), s32[]{:S(2)}) async-start(), calls=%async_computation.6 | async-start | bytes 1114112 | tf_op jit(solution)/shard_map/all_gather | solution.py:44
Sparse Core Ops, SparseCore 0:
  35.5 65.2 all-reduce.2
  103.4 38.0 all-reduce.4
  194.6 30.4 all-gather.9
  228.3 53.5 all-gather.7
  285.0 48.6 all-gather.5
  335.4 31.8 all-gather.11
  371.4 53.5 all-gather.13
where the time goes:
time: 436 us
  waiting for transfers between devices  323 us (74%)
  blocking collectives  80.2 us (18%)
  between operations  14.9 us (3%)
  matrix products  13.2 us (3%)
    all_gather x3, waiting for transfers between devices, panels(): whole_row = lax.all_gather(factor_one, GY, axis=1, tiled=True)  154 us
    psum x2, waiting for transfers between devices, spread(): array = lax.psum(array, axis)  105 us
    all_gather x2, waiting for transfers between devices, gather_axes(): filled = lax.all_gather(filled, axes[number], axis=dim, tiled=True)  62.9 us
    psum x5, blocking collectives, over_axes(): array = lax.psum(array, axis)  45.7 us
    all_gather x1, blocking collectives, local(): panel_rows = lax.all_gather(gradient, GY, axis=1, tiled=True)  26.8 us
    dot_general x4, matrix products, matmul(): jnp.dot(leading, trailing, preferred_element_type=jnp.float32, precision=...  13.2 us
  transfers between devices with their start and end apart: 7, of which 7 were waited for; matrix products, arithmetic and copies ran while one was open for 1% of the time, Pallas kernels for 0%

commit v1 on v0

--- a/solution.py
+++ b/solution.py
@@ -41,7 +41,9 @@
 
 
 def panels(factor_one, factor_two):
-    whole_row = lax.all_gather(factor_one, GY, axis=1, tiled=True)
+    whole_row = jnp.concatenate(
+        lax.all_to_all(jnp.stack([factor_one] * lax.axis_size(GY)), GY, 0, 0), axis=1
+    )
 
     def accumulate(running, shard_rows, first_row):
         matching = lax.dynamic_slice_in_dim(whole_row, first_row, shard_rows.shape[0], 1)

time: 436 us -> 312 us (0.72)
  waiting for transfers between devices: 323 us -> 139 us
  blocking collectives: 80.2 us -> 132 us
  starting transfers between devices: 0.28 us -> 12 us
    all_gather x3 -> x0, waiting for transfers between devices: 154 us -> none  [panels(): whole_row = lax.all_gather(factor_one, GY, axis=1, tiled=True)]
    all_to_all x0 -> x2, blocking collectives: none -> 51.7 us  [panels(): lax.all_to_all(jnp.stack([factor_one] * lax.axis_size(GY)), GY, 0, 0)]
    all_gather x2, waiting for transfers between devices: 62.9 us -> 17.4 us  [gather_axes(): filled = lax.all_gather(filled, axes[number], axis=dim, tiled=True)]
    all_to_all x0 -> x1, waiting for transfers between devices: none -> 16.3 us  [panels(): lax.all_to_all(jnp.stack([factor_one] * lax.axis_size(GY)), GY, 0, 0)]
    all_to_all x0 -> x1, starting transfers between devices: none -> 11.8 us  [panels(): lax.all_to_all(jnp.stack([factor_one] * lax.axis_size(GY)), GY, 0, 0)]
  transfers between devices with their start and end apart: 7 -> 5, of which waited for: 7 -> 5; matrix products, arithmetic and copies ran while one was open for 1% -> 0% of each run, Pallas kernels for 0% -> 0%
where the time goes in v1:
time: 312 us
  waiting for transfers between devices  139 us (45%)
  blocking collectives  132 us (42%)
  between operations  14.5 us (5%)
  starting transfers between devices  12 us (4%)
  matrix products  10.7 us (3%)
    psum x2, waiting for transfers between devices, spread(): array = lax.psum(array, axis)  105 us
    all_to_all x2, blocking collectives, panels(): lax.all_to_all(jnp.stack([factor_one] * lax.axis_size(GY)), GY, 0, 0)  51.7 us
    psum x5, blocking collectives, over_axes(): array = lax.psum(array, axis)  45.7 us
    all_gather x1, blocking collectives, local(): panel_rows = lax.all_gather(gradient, GY, axis=1, tiled=True)  27 us
    all_gather x2, waiting for transfers between devices, gather_axes(): filled = lax.all_gather(filled, axes[number], axis=dim, tiled=True)  17.4 us
    all_to_all x1, waiting for transfers between devices, panels(): lax.all_to_all(jnp.stack([factor_one] * lax.axis_size(GY)), GY, 0, 0)  16.3 us
    all_to_all x1, starting transfers between devices, panels(): lax.all_to_all(jnp.stack([factor_one] * lax.axis_size(GY)), GY, 0, 0)  11.8 us
    dot_general x4, matrix products, matmul(): jnp.dot(leading, trailing, preferred_element_type=jnp.float32, precision=...  10.7 us
  transfers between devices with their start and end apart: 5, of which 5 were waited for; matrix products, arithmetic and copies ran while one was open for 0% of the time, Pallas kernels for 0%

profile of v1, /device:TPU:1, one launch (start us, length us, event | category | flops | bytes accessed | tf_op | source)
XLA Modules:
  0.0 311.9 jit_solution(2755628688935235461)
XLA Ops:
  7.2 0.0 all-reduce.3.cloned.1.call-start
  7.2 27.0 %all_gather.17 = f32[128,512]{0,1:T(8,128)S(1)} all-gather(f32[128,32]{0,1:T(8,128)} %param.2), channel_id=1, replica_groups=mesh['gx_0'=8,'gx_1'=2,'gy_0'=4,'gy_1'=2,'gy_2'=2] {'gy_0','gy_1','gy_2'}, dimensions={1}, use_global_device_ids=true | all-gather | bytes 278528 | tf_op jit(solution)/shard_map/all_gather | solution.py:67
  34.2 0.7 broadcast_select_fusion
  34.9 0.0 all-reduce.3.cloned.1.call-update
  35.0 0.0 all-reduce.5.cloned.1.call-start
  35.0 65.4 %all-reduce.3.cloned.1.call-done = f32[128,512]{0,1:T(8,128)} async-done(((f32[128,512]{0,1:T(8,128)}), f32[128,512]{0,1:T(8,128)}) %all-reduce.3.cloned.1.call-update) | async-done | bytes 262160 | tf_op jit(solution)/shard_map/psum | solution.py:27
  100.4 0.0 copy-start.1
  100.4 0.0 all-reduce.5.cloned.1.call-update
  100.4 0.0 all-gather.3.cloned.1.call-start
  100.4 0.8 copy-done.1
  101.2 0.1 copy.10
  101.3 39.7 %all-reduce.5.cloned.1.call-done = f32[128,512]{0,1:T(8,128)} async-done(((f32[128,512]{0,1:T(8,128)}), f32[128,512]{0,1:T(8,128)}) %all-reduce.5.cloned.1.call-update) | async-done | bytes 262160 | tf_op jit(solution)/shard_map/psum | solution.py:27
  141.0 2.1 multiply_reduce_fusion
  143.2 14.6 %psum.51 = f32[]{:T(128)} all-reduce(f32[]{:T(128)} %get-tuple-element.8), channel_id=1, replica_groups=mesh['gx_0'=8,'gx_1'=2,'gy_0'=4,'gy_1'=2,'gy_2'=2] {'gx_0'}, use_global_device_ids=true, to_apply=%region_3.4 | all-reduce | flops 1 | bytes 8 | tf_op jit(solution)/shard_map/psum | solution.py:33
  157.7 4.4 %psum.52 = f32[]{:T(128)} all-reduce(f32[]{:T(128)} %psum.51), channel_id=1, replica_groups=mesh['gx_0'=8,'gx_1'=2,'gy_0'=4,'gy_1'=2,'gy_2'=2] {'gx_1'}, use_global_device_ids=true, to_apply=%region_4.5 | all-reduce | flops 1 | bytes 8 | tf_op jit(solution)/shard_map/psum | solution.py:33
  162.1 9.1 %psum.53 = f32[]{:T(128)} all-reduce(f32[]{:T(128)} %psum.52), channel_id=1, replica_groups=mesh['gx_0'=8,'gx_1'=2,'gy_0'=4,'gy_1'=2,'gy_2'=2] {'gy_0'}, use_global_device_ids=true, to_apply=%region_5.6 | all-reduce | flops 1 | bytes 8 | tf_op jit(solution)/shard_map/psum | solution.py:33
  171.2 5.9 %psum.54 = f32[]{:T(128)} all-reduce(f32[]{:T(128)} %psum.53), channel_id=1, replica_groups=mesh['gx_0'=8,'gx_1'=2,'gy_0'=4,'gy_1'=2,'gy_2'=2] {'gy_1'}, use_global_device_ids=true, to_apply=%region_6.7 | all-reduce | flops 1 | bytes 8 | tf_op jit(solution)/shard_map/psum | solution.py:33
  177.1 11.8 %psum.55 = f32[]{:T(128)} all-reduce(f32[]{:T(128)} %psum.54), channel_id=1, replica_groups=mesh['gx_0'=8,'gx_1'=2,'gy_0'=4,'gy_1'=2,'gy_2'=2] {'gy_2'}, use_global_device_ids=true, to_apply=%region_7.8 | all-reduce | flops 1 | bytes 8 | tf_op jit(solution)/shard_map/psum | solution.py:33
  189.5 0.1 select_subtract_fusion
  189.6 3.9 %all_gather.18 = f32[256,128]{0,1:T(8,128)} all-gather(f32[128,128]{0,1:T(8,128)S(1)} %get-tuple-element.6), channel_id=1, replica_groups=mesh['gx_0'=8,'gx_1'=2,'gy_0'=4,'gy_1'=2,'gy_2'=2] {'gx_1'}, dimensions={0}, use_global_device_ids=true | all-gather | bytes 196608 | tf_op jit(solution)/shard_map/all_gather | solution.py:15
  193.5 0.0 all-gather.3.cloned.1.call-update
  193.5 0.0 all-gather.5.cloned.1.call-start
  193.6 0.1 stack.7
  193.7 22.3 %all_to_all.15 = f32[16,128,128]{1,2,0:T(8,128)S(1)} all-to-all(f32[16,128,128]{1,2,0:T(8,128)S(1)} %stack.7), channel_id=1, replica_groups=mesh['gx_0'=8,'gx_1'=2,'gy_0'=4,'gy_1'=2,'gy_2'=2] {'gy_0','gy_1','gy_2'}, dimensions={0} | all-to-all | bytes 2097152 | tf_op jit(solution)/shard_map/all_to_all | solution.py:45
  216.0 8.8 %all-gather.3.cloned.1.call-done = f32[2048,128]{0,1:T(8,128)} async-done(((f32[256,128]{0,1:T(8,128)}), f32[2048,128]{0,1:T(8,128)}) %all-gather.3.cloned.1.call-update) | async-done | bytes 1048592 | tf_op jit(solution)/shard_map/all_gather | solution.py:15
  224.8 3.0 fusion.3
  227.9 3.9 %all_gather.20 = f32[256,128]{1,0:T(8,128)} all-gather(f32[128,128]{1,0:T(8,128)S(1)} %fusion.3), channel_id=1, replica_groups=mesh['gx_0'=8,'gx_1'=2,'gy_0'=4,'gy_1'=2,'gy_2'=2] {'gx_1'}, dimensions={0}, use_global_device_ids=true | all-gather | bytes 196608 | tf_op jit(solution)/shard_map/all_gather | solution.py:15
  231.7 0.0 all-gather.5.cloned.1.call-update
  231.8 0.1 stack.6
  231.9 29.4 %all_to_all.16 = f32[16,128,128]{1,2,0:T(8,128)S(1)} all-to-all(f32[16,128,128]{1,2,0:T(8,128)S(1)} %stack.6), channel_id=1, replica_groups=mesh['gx_0'=8,'gx_1'=2,'gy_0'=4,'gy_1'=2,'gy_2'=2] {'gy_0','gy_1','gy_2'}, dimensions={0} | all-to-all | bytes 2097152 | tf_op jit(solution)/shard_map/all_to_all | solution.py:45
  261.3 8.6 %all-gather.5.cloned.1.call-done = f32[2048,128]{1,0:T(8,128)} async-done(((f32[256,128]{1,0:T(8,128)}), f32[2048,128]{1,0:T(8,128)}) %all-gather.5.cloned.1.call-update) | async-done | bytes 1048592 | tf_op jit(solution)/shard_map/all_gather | solution.py:15
  269.8 3.0 fusion
  272.9 1.1 stack.8
  274.0 0.0 copy-start
  274.0 11.8 %all-to-all-start.2 = ((f32[16,128,128]{1,2,0:T(8,128)}), f32[16,128,128]{1,2,0:T(8,128)S(1)}, u32[]{:S(2)}, u32[]{:S(2)}) async-start(f32[16,128,128]{1,2,0:T(8,128)} %stack.8), calls=%async_computation.2 | async-start | bytes 2097152 | tf_op jit(solution)/shard_map/all_to_all | solution.py:45
  285.8 0.7 copy.12
  286.6 16.3 %all-to-all-done.2 = f32[16,128,128]{1,2,0:T(8,128)S(1)} async-done(((f32[16,128,128]{1,2,0:T(8,128)}), f32[16,128,128]{1,2,0:T(8,128)S(1)}, u32[]{:S(2)}, u32[]{:S(2)}) %all-to-all-start.2) | async-done | bytes 1048608 | tf_op jit(solution)/shard_map/all_to_all | solution.py:45
  302.9 0.0 copy-done
  302.9 2.4 fusion.4
  (1 shorter events, 0.0 us)
Async XLA Ops:
  7.2 93.2 %all-reduce.3.cloned.1.call-start = ((), (), s32[]{:S(2)}) async-start(), calls=%async_computation.3 | async-start | bytes 524288 | tf_op jit(solution)/shard_map/psum | solution.py:27
  35.0 106.1 %all-reduce.5.cloned.1.call-start = ((), (), s32[]{:S(2)}) async-start(), calls=%async_computation.4 | async-start | bytes 524288 | tf_op jit(solution)/shard_map/psum | solution.py:27
  100.4 0.8 copy-start.1
  100.4 124.4 %all-gather.3.cloned.1.call-start = ((), (), s32[]{:S(2)}) async-start(), calls=%async_computation.5 | async-start | bytes 1179648 | tf_op jit(solution)/shard_map/all_gather | solution.py:15
  193.5 76.3 %all-gather.5.cloned.1.call-start = ((), (), s32[]{:S(2)}) async-start(), calls=%async_computation.6 | async-start | bytes 1179648 | tf_op jit(solution)/shard_map/all_gather | solution.py:15
  274.0 28.9 %copy-start = (f32[2048,128]{0,1:T(8,128)S(1)}, f32[2048,128]{0,1:T(8,128)}, u32[]{:S(2)}) copy-start(f32[2048,128]{0,1:T(8,128)} %all-gather.3.cloned.1.call-done) | copy-start | bytes 3145732
  274.0 28.9 %all-to-all-start.2 = ((f32[16,128,128]{1,2,0:T(8,128)}), f32[16,128,128]{1,2,0:T(8,128)S(1)}, u32[]{:S(2)}, u32[]{:S(2)}) async-start(f32[16,128,128]{1,2,0:T(8,128)} %stack.8), calls=%async_computation.2 | async-start | bytes 2097152 | tf_op jit(solution)/shard_map/all_to_all | solution.py:45
Sparse Core Ops, SparseCore 0:
  35.1 65.2 all-reduce.2
  102.9 38.0 all-reduce.4
  193.6 31.1 all-gather.2
  231.9 37.9 all-gather.4
